TPU v7x, 32 devices: a whole 2x2x4 slice. The times are simulated.
32 devices in a mesh: dp: 8 (over z, y), expert: 2 (over core), tensor: 2 (over x).
Axes of the slice: x: 2, y: 2, z: 4, core: 2. Of those that a mesh axis runs over, the one named last changes fastest.
Arguments:
- dense_act: bfloat16 [2, 32, 512, 3584], P(None, 'dp', 'expert', 'tensor'), may hold values from -6 to 6
- dense_cot: bfloat16 [2, 32, 512, 3584], P(None, 'dp', ('expert', 'tensor')), may hold values from -6 to 6
- dense_proj_in: bfloat16 [2, 3584, 128], P(None, 'tensor'), may hold values from -0.09375 to 0.09375
- dense_proj_out: bfloat16 [2, 3584, 128], replicated, may hold values from -0.09375 to 0.09375
- expert_act: bfloat16 [32, 8, 64, 2560], P('dp', 'expert', None, 'tensor'), may hold values from -6 to 6
- expert_cot: bfloat16 [32, 8, 64, 3584], P('dp', 'expert', 'tensor'), may hold values from -6 to 6
- expert_proj_in: bfloat16 [2560, 128], P('tensor'), may hold values from -0.125 to 0.125
- expert_proj_out: bfloat16 [3584, 128], replicated, may hold values from -0.09375 to 0.09375
- dense_valid: float32 [2, 128, 128], replicated, may hold values from -0.0012207031 to 0.0012207031
- expert_valid: float32 [8, 128, 128], P('expert'), may hold values from -0.0012207031 to 0.0012207031
- domain_ids: int32 [32], P('dp'), may hold values from 0 to 63
- prior_mix: float32 [64], replicated, may hold values from 0.002 to 0.05
Outputs:
- log_mixture_weights: float32 [64], P('dp')
All inputs are finite; a program needn't handle non-finite values.
Results may differ from a plain program's by a relative error of at most 0.0003.
Values sent between devices are 32-bit elements; how exact they have to be, the bound alone decides.
A program may use at most 128 MiB of HBM per device.

v0:
```python
import jax
import jax.numpy as jnp
from jax import lax
from jax.sharding import PartitionSpec as P


def per_device(
    dense_act,
    dense_cot,
    dense_proj_in,
    dense_proj_out,
    expert_act,
    expert_cot,
    expert_proj_in,
    expert_proj_out,
    dense_valid,
    expert_valid,
    domain_ids,
    prior_mix,
):
    block = dense_act
    dense_update_vector = lax.psum_scatter(
        jnp.einsum("lmtd,ldr->tlmr", block, dense_proj_in, preferred_element_type=jnp.float32),
        "tensor",
        scatter_dimension=0,
        tiled=True,
    )
    dense_weight_matrix = jnp.einsum(
        "lmtd,ldr->tlmr", dense_cot, dense_proj_out, preferred_element_type=jnp.float32
    )
    dense_portion = jnp.einsum(
        "fquy,fquh->quyh", dense_update_vector, dense_weight_matrix, precision=lax.Precision.HIGHEST
    )
    block = expert_act
    expert_u = lax.psum_scatter(
        jnp.einsum("mecf,fr->cmer", block, expert_proj_in, preferred_element_type=jnp.float32),
        "tensor",
        scatter_dimension=0,
        tiled=True,
    )
    expert_weight_matrix = jnp.einsum(
        "mecd,dr->cmer", expert_cot, expert_proj_out, preferred_element_type=jnp.float32
    )
    expert_part = jnp.einsum(
        "cmer,cmes->mers", expert_u, expert_weight_matrix, precision=lax.Precision.HIGHEST
    )
    dense_full = lax.psum(dense_portion, ("expert", "tensor"))
    dense_score = jnp.sum(dense_full * dense_valid[:, None], axis=(0, 2, 3))
    expert_full = lax.psum(expert_part, "tensor")
    expert_local = jnp.sum(expert_full * expert_valid[None], axis=(1, 2, 3))
    score = dense_score + lax.psum(expert_local, "expert")
    domains = prior_mix.shape[0]
    onehot = (domain_ids[:, None] == jnp.arange(domains, dtype=jnp.int32)[None, :]).astype(
        jnp.float32
    )
    domain_part = jnp.dot(score, onehot, precision=lax.Precision.HIGHEST)
    share_tally_count = domains // lax.axis_size("dp")
    first_domain = lax.axis_index("dp") * share_tally_count
    previous_domain_share = lax.dynamic_slice_in_dim(prior_mix, first_domain, share_tally_count, 0)
    domain_total = lax.psum(domain_part, "dp")
    spread = jnp.sqrt(jnp.mean(domain_total * domain_total) + 1e-06)
    z_value = domain_total / spread
    mass = jnp.sum(prior_mix * jnp.exp(0.5 * z_value))
    z_share = lax.dynamic_slice_in_dim(z_value, first_domain, share_tally_count, 0)
    return jnp.log(previous_domain_share) + 0.5 * z_share - jnp.log(mass)


def solution(mesh):
    placed = (
        P(None, "dp", "expert", "tensor"),
        P(None, "dp", ("expert", "tensor"), None),
        P(None, "tensor", None),
        P(),
        P("dp", "expert", None, "tensor"),
        P("dp", "expert", "tensor", None),
        P("tensor", None),
        P(),
        P(),
        P("expert", None, None),
        P("dp"),
        P(),
    )
    return jax.shard_map(per_device, mesh=mesh, in_specs=placed, out_specs=P("dp"), check_vma=False)
```

profile of v0, /device:TPU:0, one launch (start us, length us, event | category | flops | bytes accessed | tf_op | source)
XLA Modules:
  0.0 206.4 jit_solution(693878961875852554)
XLA Ops:
  6.5 0.0 copy-start
  6.5 0.0 copy-start.3
  6.5 0.0 all-reduce.9.cloned.1.call-start
  6.5 1.7 copy-done
  8.3 1.8 convolution_bitcast_fusion.1
  10.1 1.1 copy.18
  11.2 0.0 all-reduce.9.cloned.1.call-update
  11.3 0.0 reduce-scatter.4.cloned.1.call-start
  11.3 0.0 copy-done.3
  11.3 5.6 %convolution_bitcast_fusion = f32[256,2,4,128]{0,3,2,1:T(8,128)S(1)} fusion(bf16[2,4,256,1792]{3,2,1,0:T(8,128)(2,1)} %param.12, bf16[2,1792,128]{2,1,0:T(8,128)(2,1)S(1)} %copy-done.3), kind=kOutput, calls=%fused_computation.2 | convolution fusion | flops 939524096 | bytes 9306112 | tf_op jit(solution)/shard_map/lmtd,ldr->tlmr/dot_general | solution.py:23
  16.9 26.2 %copy.29 = f32[256,2,4,128]{2,3,1,0:T(8,128)} copy(f32[256,2,4,128]{0,3,2,1:T(8,128)S(1)} %convolution_bitcast_fusion) | data formatting | bytes 2097152
  43.2 0.0 copy-start.9
  43.2 0.0 copy-start.7
  43.2 29.4 %reshape.9 = f32[256,1024]{1,0:T(8,128)} reshape(f32[256,2,128,4]{3,2,1,0:T(8,128)} %bitcast.46) | data formatting | bytes 2097152
  72.5 0.0 reduce-scatter.4.cloned.1.call-update
  72.6 0.0 all-reduce.7.cloned.1.call-start
  72.6 0.0 copy-done.9
  72.6 0.6 dynamic-slice
  73.9 0.0 copy-done.7
  73.9 0.0 copy-start.2
  73.9 3.3 %fusion.6 = f32[128,4,4,32]{0,3,2,1:T(8,128)S(1)} fusion(bf16[4,4,32,3584]{3,2,1,0:T(8,128)(2,1)} %param.17, bf16[3584,128]{1,0:T(8,128)(2,1)S(1)} %copy-done.7), kind=kOutput, calls=%fused_computation.8 | convolution fusion | flops 469762048 | bytes 4849664 | tf_op jit(solution)/shard_map/mecd,dr->cmer/dot_general | solution.py:41
  77.2 0.0 all-reduce.9.cloned.1.call-done
  77.2 1.0 constant_dynamic-slice_fusion
  78.2 2.8 %fusion.9 = f32[4,4,128,128]{3,2,1,0:T(8,128)} fusion(f32[128,4,4,32]{0,3,2,1:T(8,128)S(1)} %fusion.6, f32[32,4,4,128]{3,2,1,0:T(4,128)S(1)} %constant_dynamic-slice_fusion), kind=kOutput, calls=%fused_computation.12 | convolution fusion | flops 100663296 | bytes 1572864 | tf_op jit(solution)/shard_map/cmer,cmes->mers/dot_general | solution.py:44
  81.0 0.0 all-reduce.7.cloned.1.call-update
  81.0 0.2 all-reduce.5.cloned.1.call-start
  81.3 0.0 copy-done.2
  81.3 5.6 %fusion.2 = f32[128,2,4,128]{0,3,2,1:T(8,128)S(1)} fusion(bf16[2,4,128,3584]{3,2,1,0:T(8,128)(2,1)} %param.13, bf16[2,3584,128]{2,1,0:T(8,128)(2,1)S(1)} %copy-done.2), kind=kOutput, calls=%fused_computation.3 | convolution fusion | flops 939524096 | bytes 9699328 | tf_op jit(solution)/shard_map/lmtd,ldr->tlmr/dot_general | solution.py:28
  86.9 8.9 %reduce-scatter.4.cloned.1.call-done = f32[128,1024]{1,0:T(8,128)} async-done(((f32[256,1024]{1,0:T(8,128)}), f32[128,1024]{1,0:T(8,128)}) %reduce-scatter.4.cloned.1.call-update) | async-done | bytes 524304
  95.8 19.5 %reshape.10 = f32[128,2,128,4]{3,2,1,0:T(8,128)} reshape(f32[128,1024]{1,0:T(8,128)} %reduce-scatter.4.cloned.1.call-done) | data formatting | bytes 1048576
  115.3 0.0 copy-start.4
  115.3 0.0 copy-start.5
  115.3 0.0 copy-start.1
  115.3 13.2 %copy.16 = f32[128,2,4,128]{0,3,2,1:T(8,128)} copy(f32[128,2,4,128]{2,3,1,0:T(8,128)} %bitcast.47) | data formatting | bytes 1048576 | tf_op jit(solution)/shard_map/reduce_scatter | solution.py:22
  128.5 0.0 copy-start.8
  128.5 0.0 copy-start.6
  128.5 3.1 %fusion.12 = f32[2,4,128,128]{3,2,1,0:T(8,128)} fusion(f32[128,2,4,128]{0,3,2,1:T(8,128)} %copy.16, f32[128,2,4,128]{0,3,2,1:T(8,128)S(1)} %fusion.2), kind=kOutput, calls=%fused_computation.22 | convolution fusion | flops 201326592 | bytes 1572864 | tf_op jit(solution)/shard_map/fquy,fquh->quyh/dot_general | solution.py:31
  131.6 0.0 all-reduce.5.cloned.1.call-update
  131.6 6.7 %all-reduce.7.cloned.1.call-done = f32[4,4,128,128]{3,2,1,0:T(8,128)} async-done(((f32[4,4,128,128]{3,2,1,0:T(8,128)}), f32[4,4,128,128]{3,2,1,0:T(8,128)}) %all-reduce.7.cloned.1.call-update) | async-done | bytes 1048592 | tf_op jit(solution)/shard_map/psum | solution.py:49
  138.3 0.0 copy-done.4
  138.3 1.4 multiply_reduce_fusion
  139.7 2.4 %psum.30 = f32[4]{0:T(128)S(1)} all-reduce(f32[4]{0:T(128)S(1)} %multiply_reduce_fusion), channel_id=1, replica_groups=mesh['dp'=8,'expert'=2,'tensor'=2] {'expert'}, use_global_device_ids=true, to_apply=%region_6.0 | all-reduce | flops 4 | bytes 32 | tf_op jit(solution)/shard_map/psum | solution.py:51
  142.1 31.8 %all-reduce.5.cloned.1.call-done = f32[2,4,128,128]{3,2,1,0:T(8,128)} async-done(((f32[2,4,128,128]{3,2,1,0:T(8,128)}), f32[2,4,128,128]{3,2,1,0:T(8,128)}) %all-reduce.5.cloned.1.call-update) | async-done | bytes 524304 | tf_op jit(solution)/shard_map/psum | solution.py:47
  173.9 0.0 copy-done.5
  173.9 1.2 multiply_reduce_fusion.1
  175.1 0.0 copy-done.8
  175.1 0.2 convolution_bitcast_fusion.2
  175.3 21.3 %psum.31 = f32[64]{0:T(128)S(1)} all-reduce(f32[64]{0:T(128)S(1)} %convolution_bitcast_fusion.2), channel_id=1, replica_groups=mesh['dp'=8,'expert'=2,'tensor'=2] {'dp'}, use_global_device_ids=true, to_apply=%region_7.0 | all-reduce | flops 64 | bytes 512 | tf_op jit(solution)/shard_map/psum | solution.py:60
  196.7 0.6 multiply_reduce_fusion.3
  198.0 0.0 copy-done.6
  198.0 0.6 multiply_reduce_fusion.2
  199.3 0.6 add_subtract_fusion
  199.9 0.0 copy-done.1
Async XLA Ops:
  6.5 1.7 copy-start
  6.5 4.8 %copy-start.3 = (bf16[2,1792,128]{2,1,0:T(8,128)(2,1)S(1)}, bf16[2,1792,128]{2,1,0:T(8,128)(2,1)}, u32[]{:S(2)}) copy-start(bf16[2,1792,128]{2,1,0:T(8,128)(2,1)} %param.14) | copy-start | bytes 2752516
  6.5 70.6 %all-reduce.9.cloned.1.call-start = ((), (), s32[]{:S(2)}) async-start(), calls=%async_computation.4 | async-start | bytes 1048576
  11.3 84.6 %reduce-scatter.4.cloned.1.call-start = ((), (), s32[]{:S(2)}) async-start(), calls=%async_computation.3 | async-start | bytes 1572864
  43.2 29.4 %copy-start.9 = (u32[32]{0:T(128)S(1)}, u32[32]{0:T(128)}, u32[]{:S(2)}) copy-start(u32[32]{0:T(128)} %constant.29) | copy-start | bytes 388
  43.2 30.7 %copy-start.7 = (bf16[3584,128]{1,0:T(8,128)(2,1)S(1)}, bf16[3584,128]{1,0:T(8,128)(2,1)}, u32[]{:S(2)}) copy-start(bf16[3584,128]{1,0:T(8,128)(2,1)} %param.19) | copy-start | bytes 2752516
  72.6 65.7 %all-reduce.7.cloned.1.call-start = ((), (), s32[]{:S(2)}) async-start(), calls=%async_computation.2 | async-start | bytes 2097152 | tf_op jit(solution)/shard_map/psum | solution.py:49
  73.9 7.4 %copy-start.2 = (bf16[2,3584,128]{2,1,0:T(8,128)(2,1)S(1)}, bf16[2,3584,128]{2,1,0:T(8,128)(2,1)}, u32[]{:S(2)}) copy-start(bf16[2,3584,128]{2,1,0:T(8,128)(2,1)} %param.15) | copy-start | bytes 5505028
  81.0 92.9 %all-reduce.5.cloned.1.call-start = ((), (), s32[]{:S(2)}) async-start(), calls=%async_computation.1 | async-start | bytes 1048576 | tf_op jit(solution)/shard_map/psum | solution.py:47
  115.3 22.9 %copy-start.4 = (f32[4,128,128]{2,1,0:T(8,128)S(1)}, f32[4,128,128]{2,1,0:T(8,128)}, u32[]{:S(2)}) copy-start(f32[4,128,128]{2,1,0:T(8,128)} %param.21) | copy-start | bytes 786436
  115.3 58.6 %copy-start.5 = (f32[2,128,128]{2,1,0:T(8,128)S(1)}, f32[2,128,128]{2,1,0:T(8,128)}, u32[]{:S(2)}) copy-start(f32[2,128,128]{2,1,0:T(8,128)} %param.20) | copy-start | bytes 393220
  115.3 84.5 %copy-start.1 = (bf16[4,4,64,1280]{3,2,1,0:T(8,128)(2,1)S(1)}, bf16[4,4,64,1280]{3,2,1,0:T(8,128)(2,1)}, u32[]{:S(2)}) copy-start(bf16[4,4,64,1280]{3,2,1,0:T(8,128)(2,1)} %param.16) | copy-start | bytes 7864324
  128.5 46.6 %copy-start.8 = (s32[4]{0:T(128)S(1)}, s32[4]{0:T(128)}, u32[]{:S(2)}) copy-start(s32[4]{0:T(128)} %param.22) | copy-start | bytes 52
  128.5 69.5 %copy-start.6 = (f32[64]{0:T(128)S(1)}, f32[64]{0:T(128)}, u32[]{:S(2)}) copy-start(f32[64]{0:T(128)} %param.23) | copy-start | bytes 772
Sparse Core Ops, SparseCore 0:
  11.4 31.3 all-reduce.8
  72.7 23.1 reduce-scatter.3
  98.1 40.0 all-reduce.6
  140.5 33.4 all-reduce.4
where the time goes:
time: 207 us; the launch traced here: 206 us
  local copies, waits for them, and re-layouts  92.7 us (45%)
  waiting for transfers between devices  47.4 us (23%)
  blocking collectives  23.8 us (11%)
  matrix products  22.5 us (11%)
  between operations  15.3 us (7%)
  other arithmetic  4.44 us (2%)
    unnamed x25, local copies, waits for them, and re-layouts  78.4 us
    psum x1, waiting for transfers between devices, per_device(): dense_full = lax.psum(dense_portion, ('expert', 'tensor'))  31.8 us
    psum x1, blocking collectives, per_device(): domain_total = lax.psum(domain_part, 'dp')  21.3 us
    reduce_scatter x1, local copies, waits for them, and re-layouts, per_device(): lax.psum_scatter(jnp.einsum('lmtd,ldr->tlmr', block, dense_proj_in, prefe...  13.2 us
    unnamed x6, waiting for transfers between devices  8.98 us
    psum x1, waiting for transfers between devices, per_device(): expert_full = lax.psum(expert_part, 'tensor')  6.66 us
    dot_general x1, matrix products, per_device(): jnp.einsum('lmtd,ldr->tlmr', dense_cot, dense_proj_out, preferred_element...  5.64 us
    dot_general x1, matrix products, per_device(): jnp.einsum('lmtd,ldr->tlmr', block, dense_proj_in, preferred_element_type...  5.62 us
  transfers between devices with their start and end apart: 4, of which 3 were waited for; matrix products, arithmetic and copies ran while one was open for 54% of the time, Pallas kernels for 0%

commit v1 on v0

v1 whole, which is shorter than its diff:
```python
import functools

import jax
import jax.numpy as jnp
from jax import lax
from jax.experimental import pallas as pl
from jax.experimental.pallas import tpu as pltpu
from jax.sharding import PartitionSpec as P

MESH = pl.DeviceIdType.MESH
HIGHEST = lax.Precision.HIGHEST


def kernel(
    sizes,
    act, cot, pin, pout, eact, ecot, epin, epout, dval, evals, ids, prior,
    out,
    va, vc, vpin, vpout, vea, vec, vepin, vepout, vdv, vev, vids, vprior,
    dsend, drecv, esend, erecv, dg, eg, acc, rows,
    a_sem, c_sem, ea_sem, ec_sem, w_sem,
    ds_sem, dr_sem, es_sem, er_sem, row_send, row_recv,
):
    nd, ne, nt = sizes
    n = nd * ne * nt
    dp, ex, tx = lax.axis_index("dp"), lax.axis_index("expert"), lax.axis_index("tensor")
    me = (dp * ne + ex) * nt + tx
    layers, micro, q, rank = cot.shape[0], cot.shape[1], cot.shape[2], pin.shape[2]
    experts, qc = ecot.shape[1], ecot.shape[2]
    hidden = eact.shape[3]
    dim = ecot.shape[3]

    def split(k):
        return lax.div(k, micro), lax.rem(k, micro)

    def load_a(o, l, m):
        first = pl.multiple_of(lax.rem(tx + o, nt) * q, q)
        return pltpu.make_async_copy(act.at[l, m, pl.ds(first, q), :], va.at[o, l, m], a_sem.at[o, l, m])

    def load_ea(o, m):
        first = pl.multiple_of(lax.rem(tx + o, nt) * qc, qc)
        return pltpu.make_async_copy(eact.at[m, :, pl.ds(first, qc), :], vea.at[o, m], ea_sem.at[o, m])

    def load_c(l, m):
        return pltpu.make_async_copy(cot.at[l, m], vc.at[l, m], c_sem.at[l, m])

    def load_ec(m):
        return pltpu.make_async_copy(ecot.at[m], vec.at[m], ec_sem.at[m])

    weights = [
        pltpu.make_async_copy(src, dst, w_sem.at[i])
        for i, (src, dst) in enumerate(
            [(epin, vepin), (pin, vpin), (pout, vpout), (dval, vdv), (epout, vepout), (evals, vev), (ids, vids), (prior, vprior)]
        )
    ]
    w_epin, w_pin, w_pout, w_dval, w_epout, w_eval, w_ids, w_prior = weights

    def send_d(o, l, m):
        return pltpu.make_async_remote_copy(
            src_ref=dsend.at[o - 1, l, m], dst_ref=drecv.at[o - 1, l, m],
            send_sem=ds_sem.at[o - 1, l, m], recv_sem=dr_sem.at[o - 1, l, m],
            device_id={"dp": dp, "expert": ex, "tensor": lax.rem(tx + o, nt)}, device_id_type=MESH,
        )

    def send_e(o, m):
        return pltpu.make_async_remote_copy(
            src_ref=esend.at[o - 1, m], dst_ref=erecv.at[o - 1, m],
            send_sem=es_sem.at[o - 1, m], recv_sem=er_sem.at[o - 1, m],
            device_id={"dp": dp, "expert": ex, "tensor": lax.rem(tx + o, nt)}, device_id_type=MESH,
        )

    def peer(i):
        t = lax.rem(me + i, n)
        return {"dp": lax.div(t, ne * nt), "expert": lax.rem(lax.div(t, nt), ne), "tensor": lax.rem(t, nt)}

    w_epin.start()
    for o in range(1, nt):
        load_ea(o, 0).start()
    for m in range(1, micro):
        for o in range(1, nt):
            load_ea(o, m).start()
    w_pin.start()

    barrier = pltpu.get_barrier_semaphore()

    @pl.loop(1, n)
    def _(i):
        pl.semaphore_signal(barrier, inc=1, device_id=peer(i), device_id_type=MESH)

    acc[...] = jnp.zeros_like(acc)
    w_epin.wait()

    def expert_out(m):
        for o in range(1, nt):
            load_ea(o, m).wait()
            esend[o - 1, m] = jnp.dot(
                vea[o, m].reshape(experts * qc, hidden), vepin[...], preferred_element_type=jnp.float32
            )
        for l in range(layers):
            for o in range(1, nt):
                load_a(o, l, m).start()

    expert_out(0)
    pl.semaphore_wait(barrier, n - 1)
    for o in range(1, nt):
        send_e(o, 0).start()

    @pl.loop(1, micro)
    def _(m):
        expert_out(m)
        for o in range(1, nt):
            send_e(o, m).start()

    w_pout.start()
    w_dval.start()
    w_pin.wait()

    @pl.loop(0, layers * micro)
    def _(k):
        l, m = split(k)
        for o in range(1, nt):
            load_a(o, l, m).wait()
            dsend[o - 1, l, m] = jnp.dot(va[o, l, m], vpin[l], preferred_element_type=jnp.float32)
        load_a(0, l, m).start()
        load_c(l, m).start()
        for o in range(1, nt):
            send_d(o, l, m).start()

    w_epout.start()
    w_eval.start()
    for m in range(micro):
        load_ea(0, m).start()
        load_ec(m).start()
    w_ids.start()
    w_prior.start()
    w_pout.wait()
    w_dval.wait()

    def fold(m, value):
        acc[m] += jnp.sum(value.reshape(-1, 8, rank), axis=0)

    @pl.loop(0, layers * micro)
    def _(k):
        l, m = split(k)
        load_a(0, l, m).wait()
        load_c(l, m).wait()
        u = jnp.dot(va[0, l, m], vpin[l], preferred_element_type=jnp.float32)
        w = jnp.dot(vc[l, m], vpout[l], preferred_element_type=jnp.float32)
        g = lax.dot_general(
            w, vdv[l], (((1,), (1,)), ((), ())), precision=HIGHEST, preferred_element_type=jnp.float32
        )
        dg[l, m] = g
        fold(m, u * g)

    w_epout.wait()
    w_eval.wait()

    @pl.loop(0, micro)
    def _(m):
        load_ea(0, m).wait()
        load_ec(m).wait()
        u = jnp.dot(vea[0, m].reshape(experts * qc, hidden), vepin[...], preferred_element_type=jnp.float32)
        w = jnp.dot(vec[m].reshape(experts * qc, dim), vepout[...], preferred_element_type=jnp.float32)
        g = jnp.concatenate(
            [
                lax.dot_general(
                    w[e * qc : (e + 1) * qc], vev[e], (((1,), (1,)), ((), ())),
                    precision=HIGHEST, preferred_element_type=jnp.float32,
                )
                for e in range(experts)
            ],
            axis=0,
        )
        eg[m] = g
        fold(m, u * g)

    @pl.loop(0, micro)
    def _(m):
        for o in range(1, nt):
            send_e(o, m).wait()
            fold(m, erecv[o - 1, m] * eg[m])

    w_ids.wait()
    w_prior.wait()

    @pl.loop(0, layers * micro)
    def _(k):
        l, m = split(k)
        for o in range(1, nt):
            send_d(o, l, m).wait()
            fold(m, drecv[o - 1, l, m] * dg[l, m])

    lanes = rows.shape[2]
    lane = lax.broadcasted_iota(jnp.int32, (1, lanes), 1)
    part = jnp.zeros((1, lanes), jnp.float32)
    for m in range(micro):
        score = jnp.sum(jnp.sum(acc[m], axis=0, keepdims=True), axis=1, keepdims=True)
        part = part + jnp.where(lane == vids[m], score, 0.0)
    rows[me] = part

    def send_row(i):
        return pltpu.make_async_remote_copy(
            src_ref=rows.at[me], dst_ref=rows.at[me], send_sem=row_send, recv_sem=row_recv,
            device_id=peer(i), device_id_type=MESH,
        )

    @pl.loop(1, n)
    def _(i):
        send_row(i).start()

    others = rows.at[pl.ds(0, n - 1)]
    pltpu.make_async_copy(others, others, row_recv).wait()
    domains = prior.shape[1]
    total = jnp.sum(rows[...], axis=0)[:, :domains]
    spread = jnp.sqrt(jnp.sum(total * total, axis=1, keepdims=True) * (1.0 / domains) + 1e-06)
    z = total / spread
    mix = vprior[...]
    mass = jnp.sum(mix * jnp.exp(0.5 * z), axis=1, keepdims=True)
    out[...] = jnp.log(mix) + 0.5 * z - jnp.log(mass)
    pltpu.make_async_copy(others, others, row_send).wait()


def per_device(sizes, *args):
    (act, cot, pin, pout, eact, ecot, epin, epout, dval, evals, ids, prior) = args
    nd, ne, nt = sizes
    n = nd * ne * nt
    layers, micro, q, dim = cot.shape
    rank, feat = pin.shape[2], pin.shape[1]
    experts, qc, hidden = ecot.shape[1], ecot.shape[2], eact.shape[3]
    domains = prior.shape[0]
    lanes = -(-domains // 128) * 128
    bf, f32 = jnp.bfloat16, jnp.float32
    V, dma = pltpu.VMEM, pltpu.SemaphoreType.DMA
    logs = pl.pallas_call(
        functools.partial(kernel, sizes),
        out_shape=jax.ShapeDtypeStruct((1, domains), f32),
        in_specs=[pl.BlockSpec(memory_space=pl.ANY)] * 12,
        out_specs=pl.BlockSpec(memory_space=pltpu.VMEM),
        scratch_shapes=[
            V((nt, layers, micro, q, feat), bf),
            V((layers, micro, q, dim), bf),
            V(pin.shape, bf),
            V(pout.shape, bf),
            V((nt, micro, experts, qc, hidden), bf),
            V((micro, experts, qc, dim), bf),
            V(epin.shape, bf),
            V(epout.shape, bf),
            V(dval.shape, f32),
            V(evals.shape, f32),
            pltpu.SMEM(ids.shape, jnp.int32),
            V((1, domains), f32),
            V((nt - 1, layers, micro, q, rank), f32),
            V((nt - 1, layers, micro, q, rank), f32),
            V((nt - 1, micro, experts * qc, rank), f32),
            V((nt - 1, micro, experts * qc, rank), f32),
            V((layers, micro, q, rank), f32),
            V((micro, experts * qc, rank), f32),
            V((micro, 8, rank), f32),
            V((n, 1, lanes), f32),
            dma((nt, layers, micro)),
            dma((layers, micro)),
            dma((nt, micro)),
            dma((micro,)),
            dma((8,)),
            dma((nt - 1, layers, micro)),
            dma((nt - 1, layers, micro)),
            dma((nt - 1, micro)),
            dma((nt - 1, micro)),
            dma,
            dma,
        ],
        compiler_params=pltpu.CompilerParams(
            collective_id=0, has_side_effects=True, vmem_limit_bytes=60 * 1024 * 1024
        ),
        name="align",
    )(act, cot, pin, pout, eact, ecot, epin, epout, dval, evals, ids, prior.reshape(1, domains))
    share = domains // nd
    return lax.dynamic_slice_in_dim(logs[0], lax.axis_index("dp") * share, share, 0)


def solution(mesh):
    sizes = (mesh.shape["dp"], mesh.shape["expert"], mesh.shape["tensor"])
    placed = (
        P(None, "dp", "expert", "tensor"),
        P(None, "dp", ("expert", "tensor"), None),
        P(None, "tensor", None),
        P(),
        P("dp", "expert", None, "tensor"),
        P("dp", "expert", "tensor", None),
        P("tensor", None),
        P(),
        P(),
        P("expert", None, None),
        P("dp"),
        P(),
    )
    return jax.shard_map(
        functools.partial(per_device, sizes), mesh=mesh, in_specs=placed, out_specs=P("dp"), check_vma=False
    )
```

time: 207 us -> 32.1 us (0.16)
  local copies, waits for them, and re-layouts: 92.7 us -> 1.27 us
  waiting for transfers between devices: 47.4 us -> 0 us
  Pallas kernels: 0 us -> 30.6 us
  blocking collectives: 23.8 us -> 0 us
  matrix products: 22.5 us -> 0 us
  between operations: 15.3 us -> 0.01 us
  other arithmetic: 4.44 us -> 0 us
    unnamed x25 -> x0, local copies, waits for them, and re-layouts: 78.4 us -> none
    psum x2 -> x0, waiting for transfers between devices: 38.4 us -> none  [the longest x1 31.8 us: per_device(): dense_full = lax.psum(dense_portion, ('expert', 'tensor'))]
    pallas_call x0 -> x1, Pallas kernels: none -> 30.6 us  [per_device(): pl.pallas_call(functools.partial(kernel, sizes), out_shape=jax.ShapeDtype...]
    psum x2 -> x0, blocking collectives: 23.8 us -> none  [the longest x1 21.3 us: per_device(): domain_total = lax.psum(domain_part, 'dp')]
    dot_general x7 -> x0, matrix products: 22.5 us -> none  [the longest x1 5.64 us: per_device(): jnp.einsum('lmtd,ldr->tlmr', dense_cot, dense_proj_out, preferred_element...]
    reduce_scatter x1 -> x0, local copies, waits for them, and re-layouts: 13.2 us -> none  [per_device(): lax.psum_scatter(jnp.einsum('lmtd,ldr->tlmr', block, dense_proj_in, prefe...]
    unnamed x6 -> x0, waiting for transfers between devices: 8.98 us -> none
    reduce_sum x4 -> x0, other arithmetic: 3.84 us -> none  [the longest x1 1.43 us: per_device(): expert_local = jnp.sum(expert_full * expert_valid[None], axis=(1, 2, 3))]
  transfers between devices with their start and end apart: 4 -> 0, of which waited for: 3 -> 0; matrix products, arithmetic and copies ran while one was open for 54% -> 0% of each run, Pallas kernels for 0% -> 0%
where the time goes in v1:
time: 32.1 us; the launch traced here: 31.9 us
  Pallas kernels  30.6 us (95%)
  local copies, waits for them, and re-layouts  1.27 us (4%)
    pallas_call x1, Pallas kernels, per_device(): pl.pallas_call(functools.partial(kernel, sizes), out_shape=jax.ShapeDtype...  30.6 us
    dynamic_slice x1, local copies, waits for them, and re-layouts, per_device(): lax.dynamic_slice_in_dim(logs[0], lax.axis_index('dp') * share, share, 0)  1.27 us

profile of v1, /device:TPU:0, one launch (start us, length us, event | category | flops | bytes accessed | tf_op | source)
XLA Modules:
  0.0 31.9 jit_solution(14284520501583991369)
XLA Ops:
  0.0 30.6 %align.1 = f32[1,64]{1,0:T(1,128)} custom-call(bf16[2,4,256,1792]{3,2,1,0:T(8,128)(2,1)} %act.1, bf16[2,4,128,3584]{3,2,1,0:T(8,128)(2,1)} %cot.1, bf16[2,1792,128]{2,1,0:T(8,128)(2,1)} %pin.1, bf16[2,3584,128]{2,1,0:T(8,128)(2,1)} %pout.1, bf16[4,4,64,1280]{3,2,1,0:T(8,128)(2,1)} %eact.1, bf16[4,4,32,3584]{3,2,1,0:T(8,128)(2,1)} %ecot.1, ...), custom_call_target="tpu_custom_call" | custom-call | tf_op jit(solution)/shard_map/align/pallas_call | solution.py:233
  30.7 1.3 %dynamic-slice_bitcast_fusion = f32[8]{0:T(128)} fusion(f32[1,64]{1,0:T(1,128)} %align.1, s32[]{:T(128)S(6)} %select_n.3), kind=kLoop, calls=%fused_computation | loop fusion | bytes 68 | tf_op jit(solution)/shard_map/dynamic_slice | solution.py:277

commit v2 on v1

--- a/solution.py
+++ b/solution.py
@@ -72,6 +72,12 @@
         t = lax.rem(me + i, n)
         return {"dp": lax.div(t, ne * nt), "expert": lax.rem(lax.div(t, nt), ne), "tensor": lax.rem(t, nt)}
 
+    barrier = pltpu.get_barrier_semaphore()
+
+    @pl.loop(1, n)
+    def _(i):
+        pl.semaphore_signal(barrier, inc=1, device_id=peer(i), device_id_type=MESH)
+
     w_epin.start()
     for o in range(1, nt):
         load_ea(o, 0).start()
@@ -79,12 +85,6 @@
         for o in range(1, nt):
             load_ea(o, m).start()
     w_pin.start()
-
-    barrier = pltpu.get_barrier_semaphore()
-
-    @pl.loop(1, n)
-    def _(i):
-        pl.semaphore_signal(barrier, inc=1, device_id=peer(i), device_id_type=MESH)
 
     acc[...] = jnp.zeros_like(acc)
     w_epin.wait()

time: 32.1 us -> 31.9 us (level)
  no operation moved by 1% of the time
where the time goes in v2:
time: 31.9 us; the launch traced here: 31.8 us
  Pallas kernels  30.5 us (96%)
  local copies, waits for them, and re-layouts  1.27 us (4%)
    pallas_call x1, Pallas kernels, per_device(): pl.pallas_call(functools.partial(kernel, sizes), out_shape=jax.ShapeDtype...  30.5 us
    dynamic_slice x1, local copies, waits for them, and re-layouts, per_device(): lax.dynamic_slice_in_dim(logs[0], lax.axis_index('dp') * share, share, 0)  1.27 us

profile of v2, /device:TPU:0, one launch (start us, length us, event | category | flops | bytes accessed | tf_op | source)
XLA Modules:
  0.0 31.8 jit_solution(17670039286888215344)
XLA Ops:
  0.0 30.5 %align.1 = f32[1,64]{1,0:T(1,128)} custom-call(bf16[2,4,256,1792]{3,2,1,0:T(8,128)(2,1)} %act.1, bf16[2,4,128,3584]{3,2,1,0:T(8,128)(2,1)} %cot.1, bf16[2,1792,128]{2,1,0:T(8,128)(2,1)} %pin.1, bf16[2,3584,128]{2,1,0:T(8,128)(2,1)} %pout.1, bf16[4,4,64,1280]{3,2,1,0:T(8,128)(2,1)} %eact.1, bf16[4,4,32,3584]{3,2,1,0:T(8,128)(2,1)} %ecot.1, ...), custom_call_target="tpu_custom_call" | custom-call | tf_op jit(solution)/shard_map/align/pallas_call | solution.py:233
  30.5 1.3 %dynamic-slice_bitcast_fusion = f32[8]{0:T(128)} fusion(f32[1,64]{1,0:T(1,128)} %align.1, s32[]{:T(128)S(6)} %select_n.3), kind=kLoop, calls=%fused_computation | loop fusion | bytes 68 | tf_op jit(solution)/shard_map/dynamic_slice | solution.py:277
